TPU v7x, 128 devices: a whole 4x4x4 slice. The times are simulated.
128 devices in a mesh: genes: 64 (over z, y, x_hi, core), cols: 2 (over x_lo).
Axes of the slice: x: 4 (x_hi: 2, x_lo: 2; x = x_hi * 2 + x_lo), y: 4, z: 4, core: 2. Of those that a mesh axis runs over, the one named last changes fastest.
Arguments:
- expression: float32 [384, 40960], P(None, ('genes', 'cols')), may hold values from -200 to 200
- resample: int32 [384], replicated, may hold values from 0 to 383
- labels: int32 [40960, 300], P(('genes', 'cols')), may hold values from 0 to 1, as said below
- ref_kim: float32 [40960], P(('genes', 'cols')), may hold values from 0 to 1
Outputs:
- connectivity: float32 [40960, 300], P(('genes', 'cols'))
- preservation: float32 [2, 300], replicated
Inputs may be any that keep to these rules, and one draw needn't show every extreme that they name: `labels`: each row holds exactly one 1; every module has 32 or more genes.
All inputs are finite; a program needn't handle non-finite values.
Results may differ from a plain program's by a relative error of at most 0.0031.
Values may be sent and summed in bfloat16 or wider, within the bound.
A program may use at most 64 MiB of HBM per device.

v0:
```python
import math
import jax
import jax.numpy as jnp
from jax import lax
from jax.sharding import Mesh
from jax.sharding import PartitionSpec as P

G = 40960
GENES = ("genes_0", "genes_1", "genes_2", "genes_3")
GENES_COLS = ("genes_0", "genes_1", "genes_2", "genes_3", "cols")


def in_order(blocks, dim):
    lengths = list(blocks.shape[1:])
    lengths[dim] *= blocks.shape[0]
    return jnp.moveaxis(blocks, 0, dim).reshape(lengths)


def sent_to_all(x, axis):
    copies = jnp.broadcast_to(x, (lax.axis_size(axis), *x.shape))
    return lax.all_to_all(copies, axis, split_axis=0, concat_axis=0, tiled=True)


def gathered_copies(x, axis, dim):
    return in_order(sent_to_all(x, axis), dim)


def split_up(x, dim, count):
    before, after = (x.shape[:dim], x.shape[dim + 1 :])
    return jnp.moveaxis(x.reshape(*before, count, -1, *after), dim, 0)


def sum_at_owner(x, axis, dim):
    count = lax.axis_size(axis)
    blocks = lax.all_to_all(split_up(x, dim, count), axis, 0, 0, tiled=True)
    return jnp.sum(blocks.astype(jnp.float32), axis=0)


def one_axis_at_a_time(x, axes):
    for axis in axes:
        x = lax.psum(x, axis)
    return x


def standardize(expression, resample):
    boot = jnp.take(expression, resample, axis=0)
    centered = boot - jnp.mean(boot, axis=0, keepdims=True)
    total = jnp.sum(centered * centered, axis=0, keepdims=True)
    return (centered * lax.rsqrt(total + 1e-06)).astype(jnp.bfloat16)


def local_sums(connectivity, labels, ref_kim):
    member = labels.astype(jnp.float32)
    kim = jnp.sum(connectivity * member, axis=1)
    rowsum = jnp.sum(connectivity, axis=1)
    stacked = jnp.stack(
        [kim, kim * kim, ref_kim, ref_kim * ref_kim, kim * ref_kim, rowsum, jnp.ones_like(kim)],
        axis=1,
    )
    return jnp.dot(
        member.T, stacked, precision=lax.Precision.HIGHEST, preferred_element_type=jnp.float32
    )


def preserve(sums, total_genes):
    counts = sums[:, 6]
    mean_x = sums[:, 0] / (counts * counts)
    var_x = jnp.maximum(sums[:, 1] / (counts * counts * counts) - mean_x * mean_x, 0.0001)
    mean_y = sums[:, 2] / counts
    var_y = jnp.maximum(sums[:, 3] / counts - mean_y * mean_y, 0.01)
    cross = sums[:, 4] / (counts * counts) - mean_x * mean_y
    between = (sums[:, 5] - sums[:, 0]) / (counts * (total_genes - counts))
    density = (mean_x - between) * jnp.sqrt(counts / var_x)
    linked = cross * jnp.sqrt(counts / (var_x * var_y))
    return jnp.stack([density, linked], axis=0)


def tile_term(row_block, column_block, column_ids, module_count):
    scores = lax.dot_general(
        row_block, column_block, (((0,), (0,)), ((), ())), preferred_element_type=jnp.float32
    )
    squares = scores * scores
    adjacency = (squares * squares * squares).astype(jnp.bfloat16)
    member_block = (
        column_ids[:, None] == jnp.arange(module_count, dtype=jnp.int32)[None, :]
    ).astype(jnp.bfloat16)
    return jnp.dot(adjacency, member_block, preferred_element_type=jnp.float32)


def add_tiles(carried, row_block, piece, every_ids, shard_width, module_count):
    span_width = piece.shape[1]
    column_step = shard_width * math.gcd(span_width // shard_width, 8)
    steps_total = span_width // column_step

    def one_step(step_index, accumulated):
        columns = lax.dynamic_slice_in_dim(piece, step_index * column_step, column_step, 1)
        column_ids = lax.dynamic_slice_in_dim(every_ids, step_index * column_step, column_step, 0)
        return accumulated + tile_term(row_block, columns, column_ids, module_count)

    return lax.fori_loop(0, steps_total, one_step, carried)


def local(expression, resample, labels, ref_kim):
    scaled = standardize(expression, resample)
    module_count = labels.shape[1]
    shard_width = scaled.shape[1]
    module_ids = jnp.sum(labels * jnp.arange(module_count, dtype=jnp.int32)[None, :], axis=1)
    row_block = gathered_copies(scaled, "cols", 1)
    panel_ids = gathered_copies(module_ids, GENES, 0)
    initial = jnp.zeros((row_block.shape[1], module_count), jnp.float32)
    partial_value = add_tiles(
        initial,
        row_block,
        lax.all_gather(scaled, GENES, axis=1, tiled=True),
        panel_ids,
        shard_width,
        module_count,
    )
    connectivity = sum_at_owner(partial_value.astype(jnp.bfloat16), "cols", 0)
    sums = one_axis_at_a_time(local_sums(connectivity, labels, ref_kim), GENES_COLS)
    return (connectivity, preserve(sums, G))


def solution(mesh):
    torus = Mesh(
        mesh.devices.reshape(4, 4, 2, 2, mesh.shape["cols"]),
        ("genes_0", "genes_1", "genes_2", "genes_3", "cols"),
    )
    placed = (P(None, GENES_COLS), P(), P(GENES_COLS, None), P(GENES_COLS))
    return jax.shard_map(
        local, mesh=torus, in_specs=placed, out_specs=(P(GENES_COLS, None), P()), check_vma=False
    )
```

profile of v0, /device:TPU:2, one launch (start us, length us, event | category | flops | bytes accessed | tf_op | source)
XLA Modules:
  0.0 233.6 jit_solution(9748620751659558973)
XLA Ops:
  7.2 0.7 compare_select_fusion
  8.0 0.7 compare_and_fusion
  8.6 1.3 copy.21
  9.9 1.7 gather_fusion
  12.3 0.9 multiply_convert_fusion
  13.3 20.1 %all_to_all.16 = s32[64,1,320]{2,1,0:T(1,128)S(1)} all-to-all(s32[64,1,320]{2,1,0:T(1,128)S(1)} %broadcast_in_dim.35), channel_id=1, replica_groups=mesh['genes_0'=4,'genes_1'=4,'genes_2'=2,'genes_3'=2,'cols'=2] {'genes_0..., dimensions={0} | all-to-all | bytes 163840 | tf_op jit(solution)/shard_map/all_to_all | solution.py:21
  33.4 1.8 broadcast_in_dim.34
  35.1 4.9 %all-to-all-start = ((bf16[2,384,320]{1,2,0:T(8,128)(2,1)}), bf16[2,384,320]{1,2,0:T(8,128)(2,1)S(1)}, u32[]{:S(2)}, u32[]{:S(2)}) async-start(bf16[2,384,320]{1,2,0:T(8,128)(2,1)} %broadcast_in_dim.34), calls=%async_computation | async-start | bytes 983040 | tf_op jit(solution)/shard_map/all_to_all | solution.py:21
  40.0 0.2 reduce.1
  40.4 6.0 %all-to-all-done = bf16[2,384,320]{1,2,0:T(8,128)(2,1)S(1)} async-done(((bf16[2,384,320]{1,2,0:T(8,128)(2,1)}), bf16[2,384,320]{1,2,0:T(8,128)(2,1)S(1)}, u32[]{:S(2)}, u32[]{:S(2)}) %all-to-all-start) | async-done | bytes 491552 | tf_op jit(solution)/shard_map/all_to_all | solution.py:21
  46.4 0.3 copy.24
  46.6 69.9 %all-gather.2.cloned.1.call-done = bf16[384,20480]{0,1:T(8,128)(2,1)} async-done(((bf16[384,320]{0,1:T(8,128)(2,1)}), bf16[384,20480]{0,1:T(8,128)(2,1)}) %all-gather.2.cloned.1.call-update) | async-done | bytes 15728656 | tf_op jit(solution)/shard_map/all_gather | solution.py:114
  116.5 43.6 %while.14 = (s32[]{:T(128)}, f32[640,300]{0,1:T(8,128)S(1)}, bf16[384,20480]{0,1:T(8,128)(2,1)}, bf16[384,640]{1,0:T(8,128)(2,1)S(1)}, s32[20480]{0:T(1024)S(1)}...) while((s32[]{:T(128)}, f32[640,300]{0,1:T(8,128)S(1)}, bf16[384,20480]{0,1:T(8,128)(2,1)}, ...), condition=%wide.region_4.5_spmd.clone, body=%wide.region_3.4_spmd.clone.sunk | while | flops 2249036800 | bytes 4024477 | solution.py:100
  116.6 5.3 %fusion.32 = f32[640,300]{0,1:T(8,128)S(1)} fusion(s32[2560]{0:T(1024)S(1)} %dynamic_slice.25, bf16[384,640]{1,0:T(8,128)(2,1)S(1)} %get-tuple-element.204, bf16[384,20480]{0,1:T(8,128)(2,1)} %get-tuple-element.203, s32[]{:T(128)S(6)} %select_n.27, f32[640,300]{0,1:T(8,128)S(1)} %get-tuple-element.193, pred[]{:T(512)S(6)} %compare.3), kind=kOutput, calls=%fused_computation.7.clone.1 | convolution fusion | flops 2249036800 | bytes 4003845 | tf_op jit(solution)/shard_map/while/body/eval_jaxpr/dot_general | solution.py:87
  122.1 5.3 %fusion.32 = f32[640,300]{0,1:T(8,128)S(1)} fusion(s32[2560]{0:T(1024)S(1)} %dynamic_slice.25, bf16[384,640]{1,0:T(8,128)(2,1)S(1)} %get-tuple-element.204, bf16[384,20480]{0,1:T(8,128)(2,1)} %get-tuple-element.203, s32[]{:T(128)S(6)} %select_n.27, f32[640,300]{0,1:T(8,128)S(1)} %get-tuple-element.193, pred[]{:T(512)S(6)} %compare.3), kind=kOutput, calls=%fused_computation.7.clone.1 | convolution fusion | flops 2249036800 | bytes 4003845 | tf_op jit(solution)/shard_map/while/body/eval_jaxpr/dot_general | solution.py:87
  127.5 5.3 %fusion.32 = f32[640,300]{0,1:T(8,128)S(1)} fusion(s32[2560]{0:T(1024)S(1)} %dynamic_slice.25, bf16[384,640]{1,0:T(8,128)(2,1)S(1)} %get-tuple-element.204, bf16[384,20480]{0,1:T(8,128)(2,1)} %get-tuple-element.203, s32[]{:T(128)S(6)} %select_n.27, f32[640,300]{0,1:T(8,128)S(1)} %get-tuple-element.193, pred[]{:T(512)S(6)} %compare.3), kind=kOutput, calls=%fused_computation.7.clone.1 | convolution fusion | flops 2249036800 | bytes 4003845 | tf_op jit(solution)/shard_map/while/body/eval_jaxpr/dot_general | solution.py:87
  133.0 5.3 %fusion.32 = f32[640,300]{0,1:T(8,128)S(1)} fusion(s32[2560]{0:T(1024)S(1)} %dynamic_slice.25, bf16[384,640]{1,0:T(8,128)(2,1)S(1)} %get-tuple-element.204, bf16[384,20480]{0,1:T(8,128)(2,1)} %get-tuple-element.203, s32[]{:T(128)S(6)} %select_n.27, f32[640,300]{0,1:T(8,128)S(1)} %get-tuple-element.193, pred[]{:T(512)S(6)} %compare.3), kind=kOutput, calls=%fused_computation.7.clone.1 | convolution fusion | flops 2249036800 | bytes 4003845 | tf_op jit(solution)/shard_map/while/body/eval_jaxpr/dot_general | solution.py:87
  138.4 5.3 %fusion.32 = f32[640,300]{0,1:T(8,128)S(1)} fusion(s32[2560]{0:T(1024)S(1)} %dynamic_slice.25, bf16[384,640]{1,0:T(8,128)(2,1)S(1)} %get-tuple-element.204, bf16[384,20480]{0,1:T(8,128)(2,1)} %get-tuple-element.203, s32[]{:T(128)S(6)} %select_n.27, f32[640,300]{0,1:T(8,128)S(1)} %get-tuple-element.193, pred[]{:T(512)S(6)} %compare.3), kind=kOutput, calls=%fused_computation.7.clone.1 | convolution fusion | flops 2249036800 | bytes 4003845 | tf_op jit(solution)/shard_map/while/body/eval_jaxpr/dot_general | solution.py:87
  143.9 5.3 %fusion.32 = f32[640,300]{0,1:T(8,128)S(1)} fusion(s32[2560]{0:T(1024)S(1)} %dynamic_slice.25, bf16[384,640]{1,0:T(8,128)(2,1)S(1)} %get-tuple-element.204, bf16[384,20480]{0,1:T(8,128)(2,1)} %get-tuple-element.203, s32[]{:T(128)S(6)} %select_n.27, f32[640,300]{0,1:T(8,128)S(1)} %get-tuple-element.193, pred[]{:T(512)S(6)} %compare.3), kind=kOutput, calls=%fused_computation.7.clone.1 | convolution fusion | flops 2249036800 | bytes 4003845 | tf_op jit(solution)/shard_map/while/body/eval_jaxpr/dot_general | solution.py:87
  149.3 5.3 %fusion.32 = f32[640,300]{0,1:T(8,128)S(1)} fusion(s32[2560]{0:T(1024)S(1)} %dynamic_slice.25, bf16[384,640]{1,0:T(8,128)(2,1)S(1)} %get-tuple-element.204, bf16[384,20480]{0,1:T(8,128)(2,1)} %get-tuple-element.203, s32[]{:T(128)S(6)} %select_n.27, f32[640,300]{0,1:T(8,128)S(1)} %get-tuple-element.193, pred[]{:T(512)S(6)} %compare.3), kind=kOutput, calls=%fused_computation.7.clone.1 | convolution fusion | flops 2249036800 | bytes 4003845 | tf_op jit(solution)/shard_map/while/body/eval_jaxpr/dot_general | solution.py:87
  154.8 5.3 %fusion.32 = f32[640,300]{0,1:T(8,128)S(1)} fusion(s32[2560]{0:T(1024)S(1)} %dynamic_slice.25, bf16[384,640]{1,0:T(8,128)(2,1)S(1)} %get-tuple-element.204, bf16[384,20480]{0,1:T(8,128)(2,1)} %get-tuple-element.203, s32[]{:T(128)S(6)} %select_n.27, f32[640,300]{0,1:T(8,128)S(1)} %get-tuple-element.193, pred[]{:T(512)S(6)} %compare.3), kind=kOutput, calls=%fused_computation.7.clone.1 | convolution fusion | flops 2249036800 | bytes 4003845 | tf_op jit(solution)/shard_map/while/body/eval_jaxpr/dot_general | solution.py:87
  160.2 0.4 reshape.236
  160.6 0.8 copy.25
  161.5 5.0 %all-to-all-start.2 = ((bf16[2,320,300]{1,2,0:T(8,128)(2,1)}), bf16[2,320,300]{1,2,0:T(8,128)(2,1)S(1)}, u32[]{:S(2)}, u32[]{:S(2)}) async-start(bf16[2,320,300]{1,2,0:T(8,128)(2,1)} %copy.25), calls=%async_computation.2 | async-start | bytes 933888 | tf_op jit(solution)/shard_map/all_to_all | solution.py:35
  166.4 6.3 %all-to-all-done.2 = bf16[2,320,300]{1,2,0:T(8,128)(2,1)S(1)} async-done(((bf16[2,320,300]{1,2,0:T(8,128)(2,1)}), bf16[2,320,300]{1,2,0:T(8,128)(2,1)S(1)}, u32[]{:S(2)}, u32[]{:S(2)}) %all-to-all-start.2) | async-done | bytes 384032 | tf_op jit(solution)/shard_map/all_to_all | solution.py:35
  173.1 0.4 convolution_bitcast_fusion
  173.6 17.1 %psum.35 = f32[300,7]{0,1:T(8,128)S(1)} all-reduce(f32[300,7]{0,1:T(8,128)S(1)} %convolution_bitcast_fusion), channel_id=1, replica_groups=mesh['genes_0'=4,'genes_1'=4,'genes_2'=2,'genes_3'=2,'cols'=2] {'genes_0'}, use_global_device_ids=true, to_apply=%region_8.9 | all-reduce | flops 2100 | bytes 16800 | tf_op jit(solution)/shard_map/psum | solution.py:41
  190.7 14.9 %psum.36 = f32[300,7]{0,1:T(8,128)S(1)} all-reduce(f32[300,7]{0,1:T(8,128)S(1)} %psum.35), channel_id=1, replica_groups=mesh['genes_0'=4,'genes_1'=4,'genes_2'=2,'genes_3'=2,'cols'=2] {'genes_1'}, use_global_device_ids=true, to_apply=%region_9.10 | all-reduce | flops 2100 | bytes 16800 | tf_op jit(solution)/shard_map/psum | solution.py:41
  205.6 8.2 %psum.37 = f32[300,7]{0,1:T(8,128)S(1)} all-reduce(f32[300,7]{0,1:T(8,128)S(1)} %psum.36), channel_id=1, replica_groups=mesh['genes_0'=4,'genes_1'=4,'genes_2'=2,'genes_3'=2,'cols'=2] {'genes_2'}, use_global_device_ids=true, to_apply=%region_10.11 | all-reduce | flops 2100 | bytes 16800 | tf_op jit(solution)/shard_map/psum | solution.py:41
  213.8 3.3 %psum.38 = f32[300,7]{0,1:T(8,128)S(1)} all-reduce(f32[300,7]{0,1:T(8,128)S(1)} %psum.37), channel_id=1, replica_groups=mesh['genes_0'=4,'genes_1'=4,'genes_2'=2,'genes_3'=2,'cols'=2] {'genes_3'}, use_global_device_ids=true, to_apply=%region_11.12 | all-reduce | flops 2100 | bytes 16800 | tf_op jit(solution)/shard_map/psum | solution.py:41
  217.0 9.1 %psum.39 = f32[300,7]{0,1:T(8,128)S(1)} all-reduce(f32[300,7]{0,1:T(8,128)S(1)} %psum.38), channel_id=1, replica_groups=mesh['genes_0'=4,'genes_1'=4,'genes_2'=2,'genes_3'=2,'cols'=2] {'cols'}, use_global_device_ids=true, to_apply=%region_12.13 | all-reduce | flops 2100 | bytes 16800 | tf_op jit(solution)/shard_map/psum | solution.py:41
  226.2 0.6 pad_maximum_fusion
  (40 shorter events, 2.0 us)
Async XLA Ops:
  7.2 6.0 %copy-start = (s32[320,300]{0,1:T(8,128)S(1)}, s32[320,300]{0,1:T(8,128)}, u32[]{:S(2)}) copy-start(s32[320,300]{0,1:T(8,128)} %param.8) | copy-start | bytes 1152004
  7.2 109.3 %all-gather.2.cloned.1.call-start = ((), (), s32[]{:S(2)}) async-start(), calls=%async_computation.3 | async-start | bytes 15974400 | tf_op jit(solution)/shard_map/all_gather | solution.py:114
  35.1 11.2 %all-to-all-start = ((bf16[2,384,320]{1,2,0:T(8,128)(2,1)}), bf16[2,384,320]{1,2,0:T(8,128)(2,1)S(1)}, u32[]{:S(2)}, u32[]{:S(2)}) async-start(bf16[2,384,320]{1,2,0:T(8,128)(2,1)} %broadcast_in_dim.34), calls=%async_computation | async-start | bytes 983040 | tf_op jit(solution)/shard_map/all_to_all | solution.py:21
  116.5 49.9 %copy-start.2 = (f32[320]{0:T(512)S(1)}, f32[320]{0:T(512)}, u32[]{:S(2)}) copy-start(f32[320]{0:T(512)} %param.9) | copy-start | bytes 3844
  161.5 11.2 %all-to-all-start.2 = ((bf16[2,320,300]{1,2,0:T(8,128)(2,1)}), bf16[2,320,300]{1,2,0:T(8,128)(2,1)S(1)}, u32[]{:S(2)}, u32[]{:S(2)}) async-start(bf16[2,320,300]{1,2,0:T(8,128)(2,1)} %copy.25), calls=%async_computation.2 | async-start | bytes 933888 | tf_op jit(solution)/shard_map/all_to_all | solution.py:35
  172.9 53.8 %copy-start.1 = (f32[320,300]{0,1:T(8,128)}, f32[320,300]{0,1:T(8,128)S(1)}, u32[]{:S(2)}) copy-start(f32[320,300]{0,1:T(8,128)S(1)} %get-tuple-element.136) | copy-start | bytes 1152004
Sparse Core Ops, SparseCore 0:
  13.3 103.1 all-gather.1
where the time goes:
time: 234 us
  waiting for transfers between devices  82.2 us (35%)
  blocking collectives  72.6 us (31%)
  matrix products  43.2 us (18%)
  between operations  14.2 us (6%)
  starting transfers between devices  9.89 us (4%)
  local copies, waits for them, and re-layouts  7.35 us (3%)
  other arithmetic  4.01 us (2%)
    all_gather x1, waiting for transfers between devices, local(): lax.all_gather(scaled, GENES, axis=1, tiled=True)  69.9 us
    psum x5, blocking collectives, one_axis_at_a_time(): x = lax.psum(x, axis)  52.5 us
    dot_general x8, matrix products, tile_term(): return jnp.dot(adjacency, member_block, preferred_element_type=jnp.float32)  42.8 us
    all_to_all x1, blocking collectives, sent_to_all(): return lax.all_to_all(copies, axis, split_axis=0, concat_axis=0, tiled=True)  20.1 us
    all_to_all x1, waiting for transfers between devices, sum_at_owner(): blocks = lax.all_to_all(split_up(x, dim, count), axis, 0, 0, tiled=True)  6.29 us
    all_to_all x1, waiting for transfers between devices, sent_to_all(): return lax.all_to_all(copies, axis, split_axis=0, concat_axis=0, tiled=True)  5.99 us
    all_to_all x1, starting transfers between devices, sum_at_owner(): blocks = lax.all_to_all(split_up(x, dim, count), axis, 0, 0, tiled=True)  4.95 us
    all_to_all x1, starting transfers between devices, sent_to_all(): return lax.all_to_all(copies, axis, split_axis=0, concat_axis=0, tiled=True)  4.9 us
  transfers between devices with their start and end apart: 3, of which 3 were waited for; matrix products, arithmetic and copies ran while one was open for 1% of the time, Pallas kernels for 0%

commit v1 on v0

--- a/solution.py
+++ b/solution.py
@@ -111,7 +111,9 @@
     partial_value = add_tiles(
         initial,
         row_block,
-        lax.all_gather(scaled, GENES, axis=1, tiled=True),
+        jnp.concatenate(
+            lax.all_to_all(jnp.stack([scaled] * lax.axis_size(GENES)), GENES, 0, 0), axis=1
+        ),
         panel_ids,
         shard_width,
         module_count,

time: 234 us -> 388 us (1.66)
  waiting for transfers between devices: 82.2 us -> 211 us
  blocking collectives: 72.6 us -> 91.4 us
  starting transfers between devices: 9.89 us -> 24.2 us
  between operations: 14.2 us -> 0.8 us
  local copies, waits for them, and re-layouts: 7.35 us -> 11.9 us
    all_to_all x0 -> x1, waiting for transfers between devices: none -> 201 us  [local(): lax.all_to_all(jnp.stack([scaled] * lax.axis_size(GENES)), GENES, 0, 0)]
    all_gather x1 -> x0, waiting for transfers between devices: 69.9 us -> none  [local(): lax.all_gather(scaled, GENES, axis=1, tiled=True)]
    psum x5, blocking collectives: 52.5 us -> 81.3 us  [one_axis_at_a_time(): x = lax.psum(x, axis)]
    all_to_all x1, blocking collectives: 20.1 us -> 10.2 us  [sent_to_all(): return lax.all_to_all(copies, axis, split_axis=0, concat_axis=0, tiled=True)]
    all_to_all x0 -> x1, starting transfers between devices: none -> 5.81 us  [local(): lax.all_to_all(jnp.stack([scaled] * lax.axis_size(GENES)), GENES, 0, 0)]
    another operation x0 -> x1, local copies, waits for them, and re-layouts: none -> 5.63 us  [local(): jnp.stack([scaled] * lax.axis_size(GENES))]
    all_to_all x1, starting transfers between devices: 4.9 us -> 10.5 us  [sent_to_all(): return lax.all_to_all(copies, axis, split_axis=0, concat_axis=0, tiled=True)]
where the time goes in v1:
time: 388 us; the launch traced here: 387 us
  waiting for transfers between devices  211 us (54%)
  blocking collectives  91.4 us (24%)
  matrix products  43.2 us (11%)
  starting transfers between devices  24.2 us (6%)
  local copies, waits for them, and re-layouts  11.9 us (3%)
  other arithmetic  4.29 us (1%)
    all_to_all x1, waiting for transfers between devices, local(): lax.all_to_all(jnp.stack([scaled] * lax.axis_size(GENES)), GENES, 0, 0)  201 us
    psum x5, blocking collectives, one_axis_at_a_time(): x = lax.psum(x, axis)  81.3 us
    dot_general x8, matrix products, tile_term(): return jnp.dot(adjacency, member_block, preferred_element_type=jnp.float32)  42.8 us
    all_to_all x1, starting transfers between devices, sent_to_all(): return lax.all_to_all(copies, axis, split_axis=0, concat_axis=0, tiled=True)  10.5 us
    all_to_all x1, blocking collectives, sent_to_all(): return lax.all_to_all(copies, axis, split_axis=0, concat_axis=0, tiled=True)  10.2 us
    all_to_all x1, starting transfers between devices, sum_at_owner(): blocks = lax.all_to_all(split_up(x, dim, count), axis, 0, 0, tiled=True)  7.85 us
  transfers between devices with their start and end apart: 3, of which 3 were waited for; matrix products, arithmetic and copies ran while one was open for 1% of the time, Pallas kernels for 0%

profile of v1, /device:TPU:2, one launch (start us, length us, event | category | flops | bytes accessed | tf_op | source)
XLA Modules:
  0.0 386.9 jit_solution(4037379314416334715)
XLA Ops:
  0.6 1.1 multiply_reduce_fusion.2
  1.7 0.7 broadcast_in_dim.35
  2.4 10.5 %all-to-all-start.2 = ((s32[64,1,320]{2,1,0:T(1,128)}), s32[64,1,320]{2,1,0:T(1,128)S(1)}, u32[]{:S(2)}, u32[]{:S(2)}) async-start(s32[64,1,320]{2,1,0:T(1,128)} %broadcast_in_dim.35), calls=%async_computation.2 | async-start | bytes 196608 | tf_op jit(solution)/shard_map/all_to_all | solution.py:21
  12.9 0.7 compare_select_fusion
  13.6 0.7 compare_and_fusion
  14.3 1.3 copy.23
  15.6 1.7 gather_fusion
  18.1 4.6 %all-to-all-done.2 = s32[64,1,320]{2,1,0:T(1,128)S(1)} async-done(((s32[64,1,320]{2,1,0:T(1,128)}), s32[64,1,320]{2,1,0:T(1,128)S(1)}, u32[]{:S(2)}, u32[]{:S(2)}) %all-to-all-start.2) | async-done | bytes 81952 | tf_op jit(solution)/shard_map/all_to_all | solution.py:21
  22.8 10.2 %all_to_all.21 = bf16[2,384,320]{1,2,0:T(8,128)(2,1)S(1)} all-to-all(bf16[2,384,320]{1,2,0:T(8,128)(2,1)S(1)} %broadcast_in_dim.34), channel_id=1, replica_groups=mesh['genes_0'=4,'genes_1'=4,'genes_2'=2,'genes_3'=2,'cols'=2] {'cols'}, dimensions={0} | all-to-all | bytes 983040 | tf_op jit(solution)/shard_map/all_to_all | solution.py:21
  32.9 5.6 %stack.16 = bf16[64,384,320]{1,2,0:T(8,128)(2,1)} broadcast(bf16[384,320]{0,1:T(8,128)(2,1)S(1)} %multiply_convert_fusion), dimensions={1,2} | broadcast | bytes 15974400 | tf_op jit(solution)/shard_map/stack | solution.py:115
  38.5 5.8 %all-to-all-start = ((bf16[64,384,320]{1,2,0:T(8,128)(2,1)}), bf16[64,384,320]{1,2,0:T(8,128)(2,1)}, u32[]{:S(2)}, u32[]{:S(2)}) async-start(bf16[64,384,320]{1,2,0:T(8,128)(2,1)} %stack.16), calls=%async_computation | async-start | bytes 31457280 | tf_op jit(solution)/shard_map/all_to_all | solution.py:115
  45.0 200.6 %all-to-all-done = bf16[64,384,320]{1,2,0:T(8,128)(2,1)} async-done(((bf16[64,384,320]{1,2,0:T(8,128)(2,1)}), bf16[64,384,320]{1,2,0:T(8,128)(2,1)}, u32[]{:S(2)}, u32[]{:S(2)}) %all-to-all-start) | async-done | bytes 15728672 | tf_op jit(solution)/shard_map/all_to_all | solution.py:115
  245.5 43.7 %while.14 = (s32[]{:T(128)}, f32[640,300]{0,1:T(8,128)S(1)}, bf16[384,20480]{0,1:T(8,128)(2,1)}, bf16[384,640]{1,0:T(8,128)(2,1)S(1)}, s32[20480]{0:T(1024)S(1)}...) while((s32[]{:T(128)}, f32[640,300]{0,1:T(8,128)S(1)}, bf16[384,20480]{0,1:T(8,128)(2,1)}, ...), condition=%wide.region_4.5_spmd.clone, body=%wide.region_3.4_spmd.clone.sunk | while | flops 2249036800 | bytes 4024477 | solution.py:100
  245.6 5.4 %fusion.32 = f32[640,300]{0,1:T(8,128)S(1)} fusion(s32[2560]{0:T(1024)S(1)} %dynamic_slice.25, bf16[384,640]{1,0:T(8,128)(2,1)S(1)} %get-tuple-element.204, bf16[384,20480]{0,1:T(8,128)(2,1)} %get-tuple-element.203, s32[]{:T(128)S(6)} %select_n.29, f32[640,300]{0,1:T(8,128)S(1)} %get-tuple-element.193, pred[]{:T(512)S(6)} %compare.3), kind=kOutput, calls=%fused_computation.7.clone.1 | convolution fusion | flops 2249036800 | bytes 4003845 | tf_op jit(solution)/shard_map/while/body/eval_jaxpr/dot_general | solution.py:87
  251.1 5.3 %fusion.32 = f32[640,300]{0,1:T(8,128)S(1)} fusion(s32[2560]{0:T(1024)S(1)} %dynamic_slice.25, bf16[384,640]{1,0:T(8,128)(2,1)S(1)} %get-tuple-element.204, bf16[384,20480]{0,1:T(8,128)(2,1)} %get-tuple-element.203, s32[]{:T(128)S(6)} %select_n.29, f32[640,300]{0,1:T(8,128)S(1)} %get-tuple-element.193, pred[]{:T(512)S(6)} %compare.3), kind=kOutput, calls=%fused_computation.7.clone.1 | convolution fusion | flops 2249036800 | bytes 4003845 | tf_op jit(solution)/shard_map/while/body/eval_jaxpr/dot_general | solution.py:87
  256.6 5.3 %fusion.32 = f32[640,300]{0,1:T(8,128)S(1)} fusion(s32[2560]{0:T(1024)S(1)} %dynamic_slice.25, bf16[384,640]{1,0:T(8,128)(2,1)S(1)} %get-tuple-element.204, bf16[384,20480]{0,1:T(8,128)(2,1)} %get-tuple-element.203, s32[]{:T(128)S(6)} %select_n.29, f32[640,300]{0,1:T(8,128)S(1)} %get-tuple-element.193, pred[]{:T(512)S(6)} %compare.3), kind=kOutput, calls=%fused_computation.7.clone.1 | convolution fusion | flops 2249036800 | bytes 4003845 | tf_op jit(solution)/shard_map/while/body/eval_jaxpr/dot_general | solution.py:87
  262.0 5.3 %fusion.32 = f32[640,300]{0,1:T(8,128)S(1)} fusion(s32[2560]{0:T(1024)S(1)} %dynamic_slice.25, bf16[384,640]{1,0:T(8,128)(2,1)S(1)} %get-tuple-element.204, bf16[384,20480]{0,1:T(8,128)(2,1)} %get-tuple-element.203, s32[]{:T(128)S(6)} %select_n.29, f32[640,300]{0,1:T(8,128)S(1)} %get-tuple-element.193, pred[]{:T(512)S(6)} %compare.3), kind=kOutput, calls=%fused_computation.7.clone.1 | convolution fusion | flops 2249036800 | bytes 4003845 | tf_op jit(solution)/shard_map/while/body/eval_jaxpr/dot_general | solution.py:87
  267.5 5.3 %fusion.32 = f32[640,300]{0,1:T(8,128)S(1)} fusion(s32[2560]{0:T(1024)S(1)} %dynamic_slice.25, bf16[384,640]{1,0:T(8,128)(2,1)S(1)} %get-tuple-element.204, bf16[384,20480]{0,1:T(8,128)(2,1)} %get-tuple-element.203, s32[]{:T(128)S(6)} %select_n.29, f32[640,300]{0,1:T(8,128)S(1)} %get-tuple-element.193, pred[]{:T(512)S(6)} %compare.3), kind=kOutput, calls=%fused_computation.7.clone.1 | convolution fusion | flops 2249036800 | bytes 4003845 | tf_op jit(solution)/shard_map/while/body/eval_jaxpr/dot_general | solution.py:87
  272.9 5.3 %fusion.32 = f32[640,300]{0,1:T(8,128)S(1)} fusion(s32[2560]{0:T(1024)S(1)} %dynamic_slice.25, bf16[384,640]{1,0:T(8,128)(2,1)S(1)} %get-tuple-element.204, bf16[384,20480]{0,1:T(8,128)(2,1)} %get-tuple-element.203, s32[]{:T(128)S(6)} %select_n.29, f32[640,300]{0,1:T(8,128)S(1)} %get-tuple-element.193, pred[]{:T(512)S(6)} %compare.3), kind=kOutput, calls=%fused_computation.7.clone.1 | convolution fusion | flops 2249036800 | bytes 4003845 | tf_op jit(solution)/shard_map/while/body/eval_jaxpr/dot_general | solution.py:87
  278.4 5.3 %fusion.32 = f32[640,300]{0,1:T(8,128)S(1)} fusion(s32[2560]{0:T(1024)S(1)} %dynamic_slice.25, bf16[384,640]{1,0:T(8,128)(2,1)S(1)} %get-tuple-element.204, bf16[384,20480]{0,1:T(8,128)(2,1)} %get-tuple-element.203, s32[]{:T(128)S(6)} %select_n.29, f32[640,300]{0,1:T(8,128)S(1)} %get-tuple-element.193, pred[]{:T(512)S(6)} %compare.3), kind=kOutput, calls=%fused_computation.7.clone.1 | convolution fusion | flops 2249036800 | bytes 4003845 | tf_op jit(solution)/shard_map/while/body/eval_jaxpr/dot_general | solution.py:87
  283.8 5.3 %fusion.32 = f32[640,300]{0,1:T(8,128)S(1)} fusion(s32[2560]{0:T(1024)S(1)} %dynamic_slice.25, bf16[384,640]{1,0:T(8,128)(2,1)S(1)} %get-tuple-element.204, bf16[384,20480]{0,1:T(8,128)(2,1)} %get-tuple-element.203, s32[]{:T(128)S(6)} %select_n.29, f32[640,300]{0,1:T(8,128)S(1)} %get-tuple-element.193, pred[]{:T(512)S(6)} %compare.3), kind=kOutput, calls=%fused_computation.7.clone.1 | convolution fusion | flops 2249036800 | bytes 4003845 | tf_op jit(solution)/shard_map/while/body/eval_jaxpr/dot_general | solution.py:87
  289.3 0.4 reshape.272
  289.7 0.8 copy.27
  290.5 7.8 %all-to-all-start.3 = ((bf16[2,320,300]{1,2,0:T(8,128)(2,1)}), bf16[2,320,300]{1,2,0:T(8,128)(2,1)S(1)}, u32[]{:S(2)}, u32[]{:S(2)}) async-start(bf16[2,320,300]{1,2,0:T(8,128)(2,1)} %copy.27), calls=%async_computation.3 | async-start | bytes 933888 | tf_op jit(solution)/shard_map/all_to_all | solution.py:35
  298.4 5.7 %all-to-all-done.3 = bf16[2,320,300]{1,2,0:T(8,128)(2,1)S(1)} async-done(((bf16[2,320,300]{1,2,0:T(8,128)(2,1)}), bf16[2,320,300]{1,2,0:T(8,128)(2,1)S(1)}, u32[]{:S(2)}, u32[]{:S(2)}) %all-to-all-start.3) | async-done | bytes 384032 | tf_op jit(solution)/shard_map/all_to_all | solution.py:35
  304.5 0.4 convolution_bitcast_fusion
  304.9 16.0 %psum.35 = f32[300,7]{0,1:T(8,128)S(1)} all-reduce(f32[300,7]{0,1:T(8,128)S(1)} %convolution_bitcast_fusion), channel_id=1, replica_groups=mesh['genes_0'=4,'genes_1'=4,'genes_2'=2,'genes_3'=2,'cols'=2] {'genes_0'}, use_global_device_ids=true, to_apply=%region_8.9 | all-reduce | flops 2100 | bytes 16800 | tf_op jit(solution)/shard_map/psum | solution.py:41
  320.9 21.2 %psum.36 = f32[300,7]{0,1:T(8,128)S(1)} all-reduce(f32[300,7]{0,1:T(8,128)S(1)} %psum.35), channel_id=1, replica_groups=mesh['genes_0'=4,'genes_1'=4,'genes_2'=2,'genes_3'=2,'cols'=2] {'genes_1'}, use_global_device_ids=true, to_apply=%region_9.10 | all-reduce | flops 2100 | bytes 16800 | tf_op jit(solution)/shard_map/psum | solution.py:41
  342.1 31.7 %psum.37 = f32[300,7]{0,1:T(8,128)S(1)} all-reduce(f32[300,7]{0,1:T(8,128)S(1)} %psum.36), channel_id=1, replica_groups=mesh['genes_0'=4,'genes_1'=4,'genes_2'=2,'genes_3'=2,'cols'=2] {'genes_2'}, use_global_device_ids=true, to_apply=%region_10.11 | all-reduce | flops 2100 | bytes 16800 | tf_op jit(solution)/shard_map/psum | solution.py:41
  373.7 3.3 psum.38
  377.0 9.2 %psum.39 = f32[300,7]{0,1:T(8,128)S(1)} all-reduce(f32[300,7]{0,1:T(8,128)S(1)} %psum.38), channel_id=1, replica_groups=mesh['genes_0'=4,'genes_1'=4,'genes_2'=2,'genes_3'=2,'cols'=2] {'cols'}, use_global_device_ids=true, to_apply=%region_12.13 | all-reduce | flops 2100 | bytes 16800 | tf_op jit(solution)/shard_map/psum | solution.py:41
  386.3 0.6 pad_maximum_fusion
  (40 shorter events, 2.6 us)
Async XLA Ops:
  2.4 20.3 %all-to-all-start.2 = ((s32[64,1,320]{2,1,0:T(1,128)}), s32[64,1,320]{2,1,0:T(1,128)S(1)}, u32[]{:S(2)}, u32[]{:S(2)}) async-start(s32[64,1,320]{2,1,0:T(1,128)} %broadcast_in_dim.35), calls=%async_computation.2 | async-start | bytes 196608 | tf_op jit(solution)/shard_map/all_to_all | solution.py:21
  38.5 207.0 %all-to-all-start = ((bf16[64,384,320]{1,2,0:T(8,128)(2,1)}), bf16[64,384,320]{1,2,0:T(8,128)(2,1)}, u32[]{:S(2)}, u32[]{:S(2)}) async-start(bf16[64,384,320]{1,2,0:T(8,128)(2,1)} %stack.16), calls=%async_computation | async-start | bytes 31457280 | tf_op jit(solution)/shard_map/all_to_all | solution.py:115
  245.5 52.8 %copy-start.2 = (f32[320]{0:T(512)S(1)}, f32[320]{0:T(512)}, u32[]{:S(2)}) copy-start(f32[320]{0:T(512)} %param.9) | copy-start | bytes 3844
  245.5 58.7 %copy-start = (s32[320,300]{0,1:T(8,128)S(1)}, s32[320,300]{0,1:T(8,128)}, u32[]{:S(2)}) copy-start(s32[320,300]{0,1:T(8,128)} %param.8) | copy-start | bytes 1152004
  290.5 13.5 %all-to-all-start.3 = ((bf16[2,320,300]{1,2,0:T(8,128)(2,1)}), bf16[2,320,300]{1,2,0:T(8,128)(2,1)S(1)}, u32[]{:S(2)}, u32[]{:S(2)}) async-start(bf16[2,320,300]{1,2,0:T(8,128)(2,1)} %copy.27), calls=%async_computation.3 | async-start | bytes 933888 | tf_op jit(solution)/shard_map/all_to_all | solution.py:35
  304.3 82.6 %copy-start.1 = (f32[320,300]{0,1:T(8,128)}, f32[320,300]{0,1:T(8,128)S(1)}, u32[]{:S(2)}) copy-start(f32[320,300]{0,1:T(8,128)S(1)} %get-tuple-element.136) | copy-start | bytes 1152004
